TPU v7x, 32 devices: a whole 2x2x4 slice. The times are simulated.
32 devices in a mesh: ex: 16 (over z, y, core), ta: 2 (over x).
Axes of the slice: x: 2, y: 2, z: 4, core: 2. Of those that a mesh axis runs over, the one named last changes fastest.
Arguments:
- slot_expert: int32 [48], replicated, may hold values from 0 to 31, as said below
- gate_train: bfloat16 [32, 4096, 1024], P('ex', 'ta'), may hold values from -0.09375 to 0.09375
- up_train: bfloat16 [32, 4096, 1024], P('ex', 'ta'), may hold values from -0.09375 to 0.09375
- down_train: bfloat16 [32, 1024, 4096], P('ex', None, 'ta'), may hold values from -0.1875 to 0.1875
- slot_tokens: bfloat16 [48, 128, 4096], P('ex', None, 'ta'), may hold values from -6 to 6
Outputs:
- gate_serve: bfloat16 [48, 1024, 4096], P('ex', 'ta')
- up_serve: bfloat16 [48, 1024, 4096], P('ex', 'ta')
- down_serve: bfloat16 [48, 4096, 1024], P('ex', None, 'ta')
- expert_out: bfloat16 [48, 128, 4096], P('ex', None, 'ta')
Inputs may be any that keep to these rules, and one draw needn't show every extreme that they name: `slot_expert`: every expert 0 to 32-1 is named by at least one slot. The 3 slots of one index p of ex (slots p*3 to p*3+3-1) name experts from 3 different blocks of 2 experts (block q holds experts q*2 to q*2+2-1), so every block of experts gives every block of slots at most one expert, and exactly one for 3 blocks.
All inputs are finite; a program needn't handle non-finite values.
Results may differ from a plain program's by a relative error of at most 0.0015.
Values may be sent and summed in bfloat16 or wider, within the bound.
A program may use at most 192 MiB of HBM per device.

v0:
```python
import jax
import jax.numpy as jnp
from jax import lax
from jax.sharding import PartitionSpec as P


def for_sending(x):
    def short(part):
        return part.astype(jnp.bfloat16) if part.dtype == jnp.float32 else part

    return jax.tree.map(short, x)


def taken_in(x, axis, dim, take_in, carry):
    whole = jax.tree.map(lambda part: lax.all_gather(part, axis, axis=dim, tiled=True), x)
    return take_in(carry, whole, jnp.int32(0))


def scattered(product, span, axis):
    everything = product(jnp.int32(0), lax.axis_size(axis) * span)
    own = lax.psum_scatter(everything, axis, scatter_dimension=0, tiled=True)
    return own


def move_slots(first, second, third, slot_expert):
    spread = [
        jax.tree.map(
            lambda part, own: part.astype(own.dtype),
            lax.all_to_all(for_sending(matrix), "ex", split_axis=2, concat_axis=0, tiled=True),
            matrix,
        )
        for matrix in (first, second, third)
    ]
    wanted = slot_expert.astype(jnp.int32)
    packed = [jnp.take(matrix, wanted, axis=0) for matrix in spread]
    received = [
        jax.tree.map(
            lambda part, own: part.astype(own.dtype),
            lax.all_to_all(for_sending(matrix), "ex", split_axis=0, concat_axis=2, tiled=True),
            matrix,
        )
        for matrix in packed
    ]
    return tuple(received)


def body(slot_expert, gate_train, up_train, down_train, slot_tokens):
    down_rows = jnp.swapaxes(down_train, 1, 2)
    gate_wide, up_wide, down_wide = (
        lax.all_to_all(gate_train, "ta", split_axis=2, concat_axis=1, tiled=True),
        lax.all_to_all(up_train, "ta", split_axis=2, concat_axis=1, tiled=True),
        lax.all_to_all(down_rows, "ta", split_axis=2, concat_axis=1, tiled=True),
    )
    gate_slots, up_slots, down_serve = move_slots(gate_wide, up_wide, down_wide, slot_expert)
    gate_serve = jnp.swapaxes(gate_slots, 1, 2)
    up_serve = jnp.swapaxes(up_slots, 1, 2)
    slot_count = slot_tokens.shape[0]
    tokens_cap = slot_tokens.shape[1]
    hidden_cols = gate_serve.shape[1]
    empty = jnp.zeros((slot_count, tokens_cap, hidden_cols), jnp.float32)

    def accumulate(totals, shard_part, row_start):
        width = shard_part.shape[2]
        gate_cols = lax.dynamic_slice_in_dim(gate_serve, row_start, width, 2)
        up_cols = lax.dynamic_slice_in_dim(up_serve, row_start, width, 2)
        gate_add = jnp.einsum(
            "sck,sfk->scf", shard_part, gate_cols, preferred_element_type=jnp.float32
        )
        up_add = jnp.einsum("sck,sfk->scf", shard_part, up_cols, preferred_element_type=jnp.float32)
        return (totals[0] + gate_add, totals[1] + up_add)

    gate_act, up_act = taken_in(slot_tokens, "ta", 2, accumulate, (empty, empty))
    hidden = (jax.nn.silu(gate_act) * up_act).astype(jnp.bfloat16)

    def project(row_start, row_count):
        down_part = lax.dynamic_slice_in_dim(down_serve, row_start, row_count, 1)
        return jnp.einsum("scf,sdf->dsc", hidden, down_part, preferred_element_type=jnp.float32)

    share_rows = down_serve.shape[1] // lax.axis_size("ta")
    summed = scattered(project, share_rows, "ta")
    expert_out = jnp.transpose(summed, (1, 2, 0)).astype(jnp.bfloat16)
    return (gate_serve, up_serve, down_serve, expert_out)


def solution(mesh):
    placed = (
        P(),
        P("ex", "ta", None),
        P("ex", "ta", None),
        P("ex", None, "ta"),
        P("ex", None, "ta"),
    )
    return jax.shard_map(
        body,
        mesh=mesh,
        in_specs=placed,
        out_specs=(
            P("ex", "ta", None),
            P("ex", "ta", None),
            P("ex", None, "ta"),
            P("ex", None, "ta"),
        ),
        check_vma=False,
    )
```

profile of v0, /device:TPU:12, one launch (start us, length us, event | category | flops | bytes accessed | tf_op | source)
XLA Modules:
  0.0 1892.3 jit_solution(17709354359491364519)
XLA Ops:
  7.2 21.4 %copy.41 = bf16[2,2048,1024]{1,0,2:T(2,128)(2,1)} copy(bf16[2,2048,1024]{2,1,0:T(8,128)(2,1)} %param.8) | data formatting | bytes 16777216 | tf_op args[1]
  35.5 21.4 %copy.48 = bf16[2,2048,1024]{1,0,2:T(2,128)(2,1)} copy(bf16[2,2048,1024]{2,1,0:T(8,128)(2,1)} %param.9) | data formatting | bytes 16777216 | tf_op args[2]
  56.9 71.2 %all-to-all-done = bf16[2,2048,1024]{1,0,2:T(2,128)(2,1)} async-done(((bf16[2,2048,1024]{1,0,2:T(2,128)(2,1)}), bf16[2,2048,1024]{1,0,2:T(2,128)(2,1)}, u32[]{:S(2)}, u32[]{:S(2)}) %all-to-all-start) | async-done | bytes 8388640 | tf_op jit(solution)/shard_map/all_to_all | solution.py:50
  135.1 16.4 copy.69
  151.5 75.4 %all-to-all-done.3 = bf16[2,2048,1024]{1,0,2:T(2,128)(2,1)} async-done(((bf16[2,2048,1024]{1,0,2:T(2,128)(2,1)}), bf16[2,2048,1024]{1,0,2:T(2,128)(2,1)}, u32[]{:S(2)}, u32[]{:S(2)}) %all-to-all-start.3) | async-done | bytes 8388640 | tf_op jit(solution)/shard_map/all_to_all | solution.py:51
  233.8 10.7 copy.42
  244.4 11.4 copy.43
  255.8 21.5 %copy.44 = bf16[2,4096,512]{1,0,2:T(2,128)(2,1)} copy(bf16[2,4096,512]{2,1,0:T(8,128)(2,1)} %bitcast.74) | data formatting | bytes 16777216 | tf_op jit(solution)/shard_map/all_to_all | solution.py:50
  277.3 47.4 %all-to-all-done.6 = bf16[2,2048,1024]{1,0,2:T(2,128)(2,1)} async-done(((bf16[2,2048,1024]{1,0,2:T(2,128)(2,1)}), bf16[2,2048,1024]{1,0,2:T(2,128)(2,1)}, u32[]{:S(2)}, u32[]{:S(2)}) %all-to-all-start.6) | async-done | bytes 8388640 | tf_op jit(solution)/shard_map/all_to_all | solution.py:52
  331.5 10.7 copy.49
  342.2 11.4 copy.50
  353.6 21.3 %copy.51 = bf16[2,4096,512]{1,0,2:T(2,128)(2,1)} copy(bf16[2,4096,512]{2,1,0:T(8,128)(2,1)} %bitcast.76) | data formatting | bytes 16777216 | tf_op jit(solution)/shard_map/all_to_all | solution.py:51
  374.9 139.1 %all-to-all-done.1 = bf16[2,4096,512]{1,0,2:T(2,128)(2,1)} async-done(((bf16[2,4096,512]{1,0,2:T(2,128)(2,1)}), bf16[2,4096,512]{1,0,2:T(2,128)(2,1)}, u32[]{:S(2)}, u32[]{:S(2)}) %all-to-all-start.1) | async-done | bytes 8388640 | tf_op jit(solution)/shard_map/all_to_all | solution.py:29
  519.0 10.7 copy.56
  529.7 11.4 copy.57
  541.1 21.3 %copy.58 = bf16[2,4096,512]{1,0,2:T(2,128)(2,1)} copy(bf16[2,4096,512]{2,1,0:T(8,128)(2,1)} %bitcast.78) | data formatting | bytes 16777216 | tf_op jit(solution)/shard_map/all_to_all | solution.py:52
  562.4 139.3 %all-to-all-done.4 = bf16[2,4096,512]{1,0,2:T(2,128)(2,1)} async-done(((bf16[2,4096,512]{1,0,2:T(2,128)(2,1)}), bf16[2,4096,512]{1,0,2:T(2,128)(2,1)}, u32[]{:S(2)}, u32[]{:S(2)}) %all-to-all-start.4) | async-done | bytes 8388640 | tf_op jit(solution)/shard_map/all_to_all | solution.py:29
  706.9 12.8 copy.45
  727.5 13.0 copy.52
  748.3 9.8 gather_fusion
  758.1 9.8 gather_fusion.1
  767.9 121.5 %all-to-all-done.7 = bf16[2,4096,512]{1,0,2:T(2,128)(2,1)} async-done(((bf16[2,4096,512]{1,0,2:T(2,128)(2,1)}), bf16[2,4096,512]{1,0,2:T(2,128)(2,1)}, u32[]{:S(2)}, u32[]{:S(2)}) %all-to-all-start.7) | async-done | bytes 8388640 | tf_op jit(solution)/shard_map/all_to_all | solution.py:29
  889.4 12.8 copy.59
  919.8 17.2 broadcast_select_fusion
  937.0 277.4 %all_to_all.162 = bf16[48,4096,32]{1,2,0:T(8,128)(2,1)} all-to-all(bf16[48,4096,32]{1,2,0:T(8,128)(2,1)S(1)} %get-tuple-element.23), channel_id=1, replica_groups=mesh['ex'=16,'ta'=2] {'ex'}, dimensions={0} | all-to-all | bytes 25165824 | tf_op jit(solution)/shard_map/all_to_all | solution.py:39
  1214.5 276.7 %all_to_all.163 = bf16[48,4096,32]{1,2,0:T(8,128)(2,1)} all-to-all(bf16[48,4096,32]{1,2,0:T(8,128)(2,1)S(1)} %get-tuple-element.22), channel_id=1, replica_groups=mesh['ex'=16,'ta'=2] {'ex'}, dimensions={0} | all-to-all | bytes 25165824 | tf_op jit(solution)/shard_map/all_to_all | solution.py:39
  1497.0 12.8 copy.47
  1514.8 254.0 %all-to-all-done.8 = bf16[48,4096,32]{1,2,0:T(8,128)(2,1)} async-done(((bf16[48,4096,32]{1,2,0:T(8,128)(2,1)}), bf16[48,4096,32]{1,2,0:T(8,128)(2,1)}, u32[]{:S(2)}, u32[]{:S(2)}) %all-to-all-start.8) | async-done | bytes 12582944 | tf_op jit(solution)/shard_map/all_to_all | solution.py:39
  1768.9 10.7 copy.61
  1793.7 11.7 convolution_bitcast_fusion
  1805.4 16.6 copy.64
  1822.0 59.4 %reduce-scatter.2.cloned.1.call-done = f32[2048,3,128]{2,0,1:T(8,128)} async-done(((f32[4096,3,128]{2,0,1:T(8,128)}), f32[2048,3,128]{2,0,1:T(8,128)}) %reduce-scatter.2.cloned.1.call-update) | async-done | bytes 3145744 | tf_op jit(solution)/shard_map/reduce_scatter | solution.py:21
  (35 shorter events, 99.6 us)
Async XLA Ops:
  28.5 99.6 %all-to-all-start = ((bf16[2,2048,1024]{1,0,2:T(2,128)(2,1)}), bf16[2,2048,1024]{1,0,2:T(2,128)(2,1)}, u32[]{:S(2)}, u32[]{:S(2)}) async-start(bf16[2,2048,1024]{1,0,2:T(2,128)(2,1)} %copy.41), calls=%async_computation | async-start | bytes 16777216 | tf_op jit(solution)/shard_map/all_to_all | solution.py:50
  128.1 98.7 %all-to-all-start.3 = ((bf16[2,2048,1024]{1,0,2:T(2,128)(2,1)}), bf16[2,2048,1024]{1,0,2:T(2,128)(2,1)}, u32[]{:S(2)}, u32[]{:S(2)}) async-start(bf16[2,2048,1024]{1,0,2:T(2,128)(2,1)} %copy.48), calls=%async_computation.3 | async-start | bytes 16777216 | tf_op jit(solution)/shard_map/all_to_all | solution.py:51
  226.8 97.8 %all-to-all-start.6 = ((bf16[2,2048,1024]{1,0,2:T(2,128)(2,1)}), bf16[2,2048,1024]{1,0,2:T(2,128)(2,1)}, u32[]{:S(2)}, u32[]{:S(2)}) async-start(bf16[2,2048,1024]{1,0,2:T(2,128)(2,1)} %bitcast.72), calls=%async_computation.6 | async-start | bytes 16777216 | tf_op jit(solution)/shard_map/all_to_all | solution.py:52
  324.7 189.4 %all-to-all-start.1 = ((bf16[2,4096,512]{1,0,2:T(2,128)(2,1)}), bf16[2,4096,512]{1,0,2:T(2,128)(2,1)}, u32[]{:S(2)}, u32[]{:S(2)}) async-start(bf16[2,4096,512]{1,0,2:T(2,128)(2,1)} %copy.44), calls=%async_computation.1 | async-start | bytes 16777216 | tf_op jit(solution)/shard_map/all_to_all | solution.py:29
  514.0 187.7 %all-to-all-start.4 = ((bf16[2,4096,512]{1,0,2:T(2,128)(2,1)}), bf16[2,4096,512]{1,0,2:T(2,128)(2,1)}, u32[]{:S(2)}, u32[]{:S(2)}) async-start(bf16[2,4096,512]{1,0,2:T(2,128)(2,1)} %copy.51), calls=%async_computation.4 | async-start | bytes 16777216 | tf_op jit(solution)/shard_map/all_to_all | solution.py:29
  562.4 144.5 %copy-start.1 = (s32[48]{0:T(128)S(1)}, s32[48]{0:T(128)}, u32[]{:S(2)}) copy-start(s32[48]{0:T(128)} %param.7) | copy-start | bytes 580
  701.7 187.7 %all-to-all-start.7 = ((bf16[2,4096,512]{1,0,2:T(2,128)(2,1)}), bf16[2,4096,512]{1,0,2:T(2,128)(2,1)}, u32[]{:S(2)}, u32[]{:S(2)}) async-start(bf16[2,4096,512]{1,0,2:T(2,128)(2,1)} %copy.58), calls=%async_computation.7 | async-start | bytes 16777216 | tf_op jit(solution)/shard_map/all_to_all | solution.py:29
  1491.2 277.7 %all-to-all-start.8 = ((bf16[48,4096,32]{1,2,0:T(8,128)(2,1)}), bf16[48,4096,32]{1,2,0:T(8,128)(2,1)}, u32[]{:S(2)}, u32[]{:S(2)}) async-start(bf16[48,4096,32]{1,2,0:T(8,128)(2,1)} %get-tuple-element.21), calls=%async_computation.8 | async-start | bytes 25165824 | tf_op jit(solution)/shard_map/all_to_all | solution.py:39
  1496.2 283.4 %all-gather.2.cloned.1.call-start = ((), (), s32[]{:S(2)}) async-start(), calls=%async_computation.10 | async-start | bytes 4718592 | tf_op jit(solution)/shard_map/all_gather | solution.py:15
  1496.9 384.5 %reduce-scatter.2.cloned.1.call-start = ((), (), s32[]{:S(2)}) async-start(), calls=%async_computation.11 | async-start | bytes 9437184 | tf_op jit(solution)/shard_map/reduce_scatter | solution.py:21
  1497.0 12.8 slice-start
  1497.0 12.8 slice-start.1
  1497.0 12.8 slice-start.2
  1779.5 7.5 copy-start
Sparse Core Ops, SparseCore 0:
  1498.5 44.7 all-gather.1
  1805.5 75.8 reduce-scatter.1
where the time goes:
time: 1900 us; the launch traced here: 1890 us
  waiting for transfers between devices  908 us (48%)
  blocking collectives  554 us (29%)
  local copies, waits for them, and re-layouts  328 us (17%)
  starting transfers between devices  43 us (2%)
  matrix products  25.8 us (1%)
  other arithmetic  19.3 us (1%)
    all_to_all x2, blocking collectives, move_slots(): lax.all_to_all(for_sending(matrix), 'ex', split_axis=0, concat_axis=2, ti...  554 us
    all_to_all x3, waiting for transfers between devices, move_slots(): lax.all_to_all(for_sending(matrix), 'ex', split_axis=2, concat_axis=0, ti...  400 us
    all_to_all x1, waiting for transfers between devices, move_slots(): lax.all_to_all(for_sending(matrix), 'ex', split_axis=0, concat_axis=2, ti...  254 us
    unnamed x15, local copies, waits for them, and re-layouts  77.3 us
    all_to_all x1, waiting for transfers between devices, body(): lax.all_to_all(up_train, 'ta', split_axis=2, concat_axis=1, tiled=True)  75.4 us
    all_to_all x1, waiting for transfers between devices, body(): lax.all_to_all(gate_train, 'ta', split_axis=2, concat_axis=1, tiled=True)  71.2 us
    all_to_all x6, local copies, waits for them, and re-layouts, move_slots(): lax.all_to_all(for_sending(matrix), 'ex', split_axis=2, concat_axis=0, ti...  61.9 us
    reduce_scatter x1, waiting for transfers between devices, scattered(): own = lax.psum_scatter(everything, axis, scatter_dimension=0, tiled=True)  59.4 us
  transfers between devices with their start and end apart: 9, of which 8 were waited for; matrix products, arithmetic and copies ran while one was open for 14% of the time, Pallas kernels for 0%

commit v1 on v0

v1 whole, which is shorter than its diff:
```python
import jax
import jax.numpy as jnp
from jax import lax
from jax.sharding import PartitionSpec as P


def swap_over(x, axis, split, concat):
    size = lax.axis_size(axis)
    me = lax.axis_index(axis)
    width = x.shape[split] // size
    length = x.shape[concat]
    shape = list(x.shape)
    shape[split] = width
    shape[concat] = length * size
    out = jnp.zeros(shape, x.dtype)
    for shift in range(size):
        target = lax.rem(me + shift, size)
        source = lax.rem(me - shift + size, size)
        block = lax.dynamic_slice_in_dim(x, target * width, width, split)
        if shift:
            block = lax.ppermute(block, axis, [(i, (i + shift) % size) for i in range(size)])
        out = lax.dynamic_update_slice_in_dim(out, block, source * length, concat)
    return out


def spread(x):
    size = lax.axis_size("ex")
    local, rows, cols = x.shape
    parts = jnp.swapaxes(x.reshape(local, size, rows // size, cols), 0, 1)
    got = lax.all_to_all(parts, "ex", split_axis=0, concat_axis=0, tiled=True)
    return got.reshape(size * local, rows // size, cols)


def deliver(x, wanted):
    size = lax.axis_size("ex")
    rows, cols = x.shape[1:]
    packed = x.at[wanted].get(mode="promise_in_bounds")
    packed = packed.reshape(size, -1, rows, cols)
    got = lax.all_to_all(packed, "ex", split_axis=0, concat_axis=0, tiled=True)
    return jnp.swapaxes(got, 0, 1).reshape(-1, size * rows, cols)


def after(x, earlier):
    return lax.optimization_barrier((x, earlier))


def body(slot_expert, gate_train, up_train, down_train, slot_tokens):
    wanted = slot_expert.astype(jnp.int32)
    down_rows = jnp.swapaxes(down_train, 1, 2)
    gate_wide = swap_over(jnp.swapaxes(gate_train, 1, 2), "ta", 1, 2)
    up_wide = swap_over(jnp.swapaxes(up_train, 1, 2), "ta", 1, 2)
    tokens = lax.all_gather(slot_tokens, "ta", axis=2, tiled=True)

    down_spread = spread(down_rows)
    gate_wide, down_spread = after(gate_wide, down_spread)
    gate_spread = spread(gate_wide)
    up_wide, gate_spread = after(up_wide, gate_spread)
    up_spread = spread(up_wide)

    down_spread, up_spread = after(down_spread, up_spread)
    down_slots = deliver(down_spread, wanted)
    gate_spread, down_slots = after(gate_spread, down_slots)
    gate_serve = deliver(gate_spread, wanted)
    down_serve = swap_over(down_slots, "ta", 2, 1)
    up_spread, gate_serve = after(up_spread, gate_serve)
    up_serve = deliver(up_spread, wanted)

    gate_act = jnp.einsum("sck,sfk->scf", tokens, gate_serve, preferred_element_type=jnp.float32)
    up_act = jnp.einsum("sck,sfk->scf", tokens, up_serve, preferred_element_type=jnp.float32)
    hidden = (jax.nn.silu(gate_act) * up_act).astype(jnp.bfloat16)
    hidden = lax.all_gather(hidden, "ta", axis=2, tiled=True)
    expert_out = jnp.einsum(
        "scf,sdf->scd", hidden, down_slots, preferred_element_type=jnp.float32
    ).astype(jnp.bfloat16)
    return (gate_serve, up_serve, down_serve, expert_out)


def solution(mesh):
    placed = (
        P(),
        P("ex", "ta", None),
        P("ex", "ta", None),
        P("ex", None, "ta"),
        P("ex", None, "ta"),
    )
    return jax.shard_map(
        body,
        mesh=mesh,
        in_specs=placed,
        out_specs=(
            P("ex", "ta", None),
            P("ex", "ta", None),
            P("ex", None, "ta"),
            P("ex", None, "ta"),
        ),
        check_vma=False,
    )
```

time: 1900 us -> 1520 us (0.80)
  waiting for transfers between devices: 908 us -> 723 us
  local copies, waits for them, and re-layouts: 328 us -> 165 us
  other arithmetic: 19.3 us -> 0.01 us
    all_to_all x7 -> x4, waiting for transfers between devices: 848 us -> 396 us  [the longest x3 328 us: spread(): got = lax.all_to_all(parts, 'ex', split_axis=0, concat_axis=0, tiled=True)]
    ppermute x0 -> x3, waiting for transfers between devices: none -> 327 us  [swap_over(): lax.ppermute(block, axis, [(i, (i + shift) % size) for i in range(size)])]
    all_to_all x18 -> x0, local copies, waits for them, and re-layouts: 221 us -> none  [the longest x6 61.9 us: move_slots(): lax.all_to_all(for_sending(matrix), 'ex', split_axis=2, concat_axis=0, ti...]
    reduce_scatter x1 -> x0, waiting for transfers between devices: 59.4 us -> none  [scattered(): own = lax.psum_scatter(everything, axis, scatter_dimension=0, tiled=True)]
    transpose x0 -> x6, local copies, waits for them, and re-layouts: none -> 41.2 us  [the longest x3 24.1 us: spread(): parts = jnp.swapaxes(x.reshape(local, size, rows // size, cols), 0, 1)]
    unnamed x15, local copies, waits for them, and re-layouts: 77.3 us -> 36.9 us
    all_to_all x7 -> x4, starting transfers between devices: 42.9 us -> 21.5 us  [the longest x3 16.5 us: spread(): got = lax.all_to_all(parts, 'ex', split_axis=0, concat_axis=0, tiled=True)]
    another operation x0 -> x3, local copies, waits for them, and re-layouts: none -> 21.1 us
  transfers between devices with their start and end apart: 9 -> 8, of which waited for: 8 -> 7; matrix products, arithmetic and copies ran while one was open for 14% -> 6% of each run, Pallas kernels for 0% -> 0%
where the time goes in v1:
time: 1520 us
  waiting for transfers between devices  723 us (48%)
  blocking collectives  566 us (37%)
  local copies, waits for them, and re-layouts  165 us (11%)
  starting transfers between devices  26.2 us (2%)
  matrix products  24.9 us (2%)
    all_to_all x2, blocking collectives, deliver(): got = lax.all_to_all(packed, 'ex', split_axis=0, concat_axis=0, tiled=True)  554 us
    all_to_all x3, waiting for transfers between devices, spread(): got = lax.all_to_all(parts, 'ex', split_axis=0, concat_axis=0, tiled=True)  328 us
    ppermute x3, waiting for transfers between devices, swap_over(): lax.ppermute(block, axis, [(i, (i + shift) % size) for i in range(size)])  327 us
    all_to_all x1, waiting for transfers between devices, deliver(): got = lax.all_to_all(packed, 'ex', split_axis=0, concat_axis=0, tiled=True)  68.5 us
    unnamed x15, local copies, waits for them, and re-layouts  36.9 us
  transfers between devices with their start and end apart: 8, of which 7 were waited for; matrix products, arithmetic and copies ran while one was open for 6% of the time, Pallas kernels for 0%

profile of v1, /device:TPU:12, one launch (start us, length us, event | category | flops | bytes accessed | tf_op | source)
XLA Modules:
  0.0 1520.2 jit_solution(8576247654423899963)
XLA Ops:
  7.2 11.8 copy.31
  19.0 8.4 copy.32
  27.4 6.2 all-to-all-start
  33.6 12.2 constant_dynamic-slice_fusion.1
  45.8 6.3 copy.43
  53.6 6.3 copy.42
  66.6 78.4 %collective-permute-done = bf16[2,512,2048]{2,1,0:T(8,128)(2,1)} collective-permute-done((bf16[2,512,2048]{2,1,0:T(8,128)(2,1)}, bf16[2,512,2048]{2,1,0:T(8,128)(2,1)}, u32[]{:S(2)}, u32[]{:S(2)}) %collective-permute-start) | collective-permute-done | bytes 4194336 | tf_op jit(solution)/shard_map/ppermute | solution.py:21
  149.8 66.5 %all-to-all-done = bf16[16,2,128,1024]{3,2,1,0:T(8,128)(2,1)} async-done(((bf16[16,2,128,1024]{3,2,1,0:T(8,128)(2,1)}), bf16[16,2,128,1024]{3,2,1,0:T(8,128)(2,1)}, u32[]{:S(2)}, u32[]{:S(2)}) %all-to-all-start) | async-done | bytes 8388640 | tf_op jit(solution)/shard_map/all_to_all | solution.py:30
  216.3 7.9 copy.35
  229.2 6.3 copy.45
  237.0 6.2 copy.44
  249.9 78.5 %collective-permute-done.1 = bf16[2,512,2048]{2,1,0:T(8,128)(2,1)} collective-permute-done((bf16[2,512,2048]{2,1,0:T(8,128)(2,1)}, bf16[2,512,2048]{2,1,0:T(8,128)(2,1)}, u32[]{:S(2)}, u32[]{:S(2)}) %collective-permute-start.1) | collective-permute-done | bytes 4194336 | tf_op jit(solution)/shard_map/ppermute | solution.py:21
  333.2 78.7 %all-to-all-done.1 = bf16[16,2,32,4096]{3,2,1,0:T(8,128)(2,1)} async-done(((bf16[16,2,32,4096]{3,2,1,0:T(8,128)(2,1)}), bf16[16,2,32,4096]{3,2,1,0:T(8,128)(2,1)}, u32[]{:S(2)}, u32[]{:S(2)}) %all-to-all-start.1) | async-done | bytes 8388640 | tf_op jit(solution)/shard_map/all_to_all | solution.py:30
  411.8 7.9 copy.36
  419.7 5.2 all-to-all-start.2
  424.9 182.6 %all-to-all-done.2 = bf16[16,2,32,4096]{3,2,1,0:T(8,128)(2,1)} async-done(((bf16[16,2,32,4096]{3,2,1,0:T(8,128)(2,1)}), bf16[16,2,32,4096]{3,2,1,0:T(8,128)(2,1)}, u32[]{:S(2)}, u32[]{:S(2)}) %all-to-all-start.2) | async-done | bytes 8388640 | tf_op jit(solution)/shard_map/all_to_all | solution.py:30
  607.6 9.8 gather_fusion
  617.4 277.6 %all_to_all.30 = bf16[16,3,128,1024]{3,2,1,0:T(8,128)(2,1)S(1)} all-to-all(bf16[16,3,128,1024]{3,2,1,0:T(8,128)(2,1)} %bitcast.50), channel_id=1, replica_groups=mesh['ex'=16,'ta'=2] {'ex'}, dimensions={0} | all-to-all | bytes 25165824 | tf_op jit(solution)/shard_map/all_to_all | solution.py:39
  894.9 5.2 copy.37
  900.1 9.8 gather_fusion.1
  909.9 276.9 %all_to_all.31 = bf16[16,3,32,4096]{3,2,1,0:T(8,128)(2,1)S(1)} all-to-all(bf16[16,3,32,4096]{3,2,1,0:T(8,128)(2,1)} %bitcast.51), channel_id=1, replica_groups=mesh['ex'=16,'ta'=2] {'ex'}, dimensions={0} | all-to-all | bytes 25165824 | tf_op jit(solution)/shard_map/all_to_all | solution.py:39
  1191.8 9.8 gather_fusion.2
  1206.9 5.8 broadcast_in_dim.9
  1212.6 11.0 constant_dynamic-slice_fusion
  1225.1 170.0 %collective-permute-done.2 = bf16[3,2048,512]{2,1,0:T(8,128)(2,1)} collective-permute-done((bf16[3,2048,512]{2,1,0:T(8,128)(2,1)}, bf16[3,2048,512]{2,1,0:T(8,128)(2,1)}, u32[]{:S(2)}, u32[]{:S(2)}) %collective-permute-start.2) | collective-permute-done | bytes 6291488 | tf_op jit(solution)/shard_map/ppermute | solution.py:21
  1395.2 5.9 constant_dynamic-update-slice_fusion
  1401.1 9.8 convolution_bitcast_fusion.1
  1410.8 68.5 %all-to-all-done.5 = bf16[16,3,32,4096]{3,2,1,0:T(8,128)(2,1)} async-done(((bf16[16,3,32,4096]{3,2,1,0:T(8,128)(2,1)}), bf16[16,3,32,4096]{3,2,1,0:T(8,128)(2,1)}, u32[]{:S(2)}, u32[]{:S(2)}) %all-to-all-start.5) | async-done | bytes 12582944 | tf_op jit(solution)/shard_map/all_to_all | solution.py:39
  1479.3 6.8 copy.39
  1486.1 5.1 fusion.1
  1491.3 12.0 all_gather.7
  1503.3 10.0 convolution_convert_fusion
  (27 shorter events, 43.0 us)
Async XLA Ops:
  27.4 188.9 %all-to-all-start = ((bf16[16,2,128,1024]{3,2,1,0:T(8,128)(2,1)}), bf16[16,2,128,1024]{3,2,1,0:T(8,128)(2,1)}, u32[]{:S(2)}, u32[]{:S(2)}) async-start(bf16[16,2,128,1024]{3,2,1,0:T(8,128)(2,1)} %copy.32), calls=%async_computation | async-start | bytes 16777216 | tf_op jit(solution)/shard_map/all_to_all | solution.py:30
  52.1 92.9 %collective-permute-start = (bf16[2,512,2048]{2,1,0:T(8,128)(2,1)}, bf16[2,512,2048]{2,1,0:T(8,128)(2,1)}, u32[]{:S(2)}, u32[]{:S(2)}) collective-permute-start(bf16[2,512,2048]{2,1,0:T(8,128)(2,1)} %bitcast.55), channel_id=1, source_target_pairs={{0,1},{1,0},{2,3},{3,2},{4,5},{5,4},{6,7},{7,6},{8,9},{9,8},{10,11... | collective-permute-start | bytes 12582920 | tf_op jit(solution)/shard_map/ppermute | solution.py:21
  59.9 4.4 copy-start
  224.1 187.7 %all-to-all-start.1 = ((bf16[16,2,32,4096]{3,2,1,0:T(8,128)(2,1)}), bf16[16,2,32,4096]{3,2,1,0:T(8,128)(2,1)}, u32[]{:S(2)}, u32[]{:S(2)}) async-start(bf16[16,2,32,4096]{3,2,1,0:T(8,128)(2,1)} %copy.35), calls=%async_computation.1 | async-start | bytes 16777216 | tf_op jit(solution)/shard_map/all_to_all | solution.py:30
  235.5 92.9 %collective-permute-start.1 = (bf16[2,512,2048]{2,1,0:T(8,128)(2,1)}, bf16[2,512,2048]{2,1,0:T(8,128)(2,1)}, u32[]{:S(2)}, u32[]{:S(2)}) collective-permute-start(bf16[2,512,2048]{2,1,0:T(8,128)(2,1)} %bitcast.56), channel_id=1, source_target_pairs={{0,1},{1,0},{2,3},{3,2},{4,5},{5,4},{6,7},{7,6},{8,9},{9,8},{10,11... | collective-permute-start | bytes 12582920 | tf_op jit(solution)/shard_map/ppermute | solution.py:21
  243.2 4.4 copy-start.1
  419.7 5.2 copy-start.4
  419.7 187.8 %all-to-all-start.2 = ((bf16[16,2,32,4096]{3,2,1,0:T(8,128)(2,1)}), bf16[16,2,32,4096]{3,2,1,0:T(8,128)(2,1)}, u32[]{:S(2)}, u32[]{:S(2)}) async-start(bf16[16,2,32,4096]{3,2,1,0:T(8,128)(2,1)} %copy.36), calls=%async_computation.2 | async-start | bytes 16777216 | tf_op jit(solution)/shard_map/all_to_all | solution.py:30
  1201.6 277.7 %all-to-all-start.5 = ((bf16[16,3,32,4096]{3,2,1,0:T(8,128)(2,1)}), bf16[16,3,32,4096]{3,2,1,0:T(8,128)(2,1)}, u32[]{:S(2)}, u32[]{:S(2)}) async-start(bf16[16,3,32,4096]{3,2,1,0:T(8,128)(2,1)} %bitcast.49), calls=%async_computation.5 | async-start | bytes 25165824 | tf_op jit(solution)/shard_map/all_to_all | solution.py:39
  1206.6 194.4 %all-gather.2.cloned.1.call-start = ((), (), s32[]{:S(2)}) async-start(), calls=%async_computation.6 | async-start | bytes 4718592 | tf_op jit(solution)/shard_map/all_gather | solution.py:52
  1223.6 171.6 %collective-permute-start.2 = (bf16[3,2048,512]{2,1,0:T(8,128)(2,1)}, bf16[3,2048,512]{2,1,0:T(8,128)(2,1)}, u32[]{:S(2)}, u32[]{:S(2)}) collective-permute-start(bf16[3,2048,512]{2,1,0:T(8,128)(2,1)} %get-tuple-element.24), channel_id=1, source_target_pairs={{0,1},{1,0},{2,3},{3,2},{4,5},{5,4},{6,7},{7,6},{8,9},{9,8},{10,11... | collective-permute-start | bytes 18874376 | tf_op jit(solution)/shard_map/ppermute | solution.py:21
  1479.3 6.8 copy-start.3
  1486.1 5.2 copy-start.2
Sparse Core Ops, SparseCore 0:
  1225.2 78.8 all-gather.1
